TPU v7x, 32 devices: a whole 2x2x4 slice. The times are simulated.
32 devices in a mesh: leaf: 4 (over y, core), grid: 8 (over z, x).
Axes of the slice: x: 2, y: 2, z: 4, core: 2. Of those that a mesh axis runs over, the one named last changes fastest.
Arguments:
- ainv_sep: bfloat16 [4, 2048, 2048], P('leaf', 'grid'), may hold values from -6 to 6
- l_panel: bfloat16 [4, 2048, 512], P('leaf', 'grid'), may hold values from -0.125 to 0.125
- block_mask: int32 [4, 1, 4], P('leaf'), may hold values 0 or 1
- owner: int32 [4, 4], P('leaf'), may hold values 0 or 1
- dinv: float32 [4, 512, 512], P('leaf', 'grid'), may hold values from -6 to 6
Outputs:
- ainv_panel: bfloat16 [4, 2048, 512], P('leaf', 'grid')
- ainv_upper: bfloat16 [4, 512, 2048], P('leaf', 'grid')
- ainv_diag: float32 [4, 512, 512], P('leaf', 'grid')
All inputs are finite; a program needn't handle non-finite values. No bound on the sum of `block_mask` or of `owner` on one device may be relied on, other than what follows from the above.
Results may differ from a plain program's by a relative error of at most 0.0019.
Values may be sent and summed in bfloat16 or wider, within the bound.
A program may use at most 128 MiB of HBM per device.

v0:
```python
import jax
import jax.numpy as jnp
from jax import lax
from jax.sharding import PartitionSpec as P

B = 512


def swapped(array, axis, stride):
    return lax.ppermute(array, axis, [(i, i ^ 1 << stride) for i in range(lax.axis_size(axis))])


def body(ainv_sep, l_panel, block_mask, owner, dinv):
    strip_rows = ainv_sep.shape[1]
    block_count = block_mask.shape[2]
    sibling = swapped(ainv_sep, "leaf", 0)
    colmask = jnp.repeat(owner[0], B)
    mixed = jnp.where(colmask[None, :] == 1, sibling[0], ainv_sep[0])
    first_row = lax.axis_index("grid") * strip_rows
    row_block = (first_row + jnp.arange(strip_rows, dtype=jnp.int32)) // B
    onehot = (row_block[:, None] == jnp.arange(block_count, dtype=jnp.int32)[None, :]).astype(
        jnp.float32
    )
    row_flags = jnp.dot(
        onehot, block_mask[0].T.astype(jnp.float32), preferred_element_type=jnp.float32
    )
    flags_wide = jnp.repeat(row_flags, B, axis=1)
    masked = jnp.where(flags_wide > 0.5, l_panel[0], jnp.zeros((), jnp.bfloat16))
    whole_panel = lax.all_gather(masked, "grid", axis=0, tiled=True)
    panel = (-jnp.dot(mixed, whole_panel, preferred_element_type=jnp.float32)).astype(jnp.bfloat16)
    upper = lax.all_to_all(panel.T, "grid", split_axis=0, concat_axis=1, tiled=True)
    diag = dinv[0] - jnp.dot(upper, whole_panel, preferred_element_type=jnp.float32)
    return (panel[None], upper[None], diag[None])


def solution(mesh):
    placed = (
        P("leaf", "grid", None),
        P("leaf", "grid", None),
        P("leaf", None, None),
        P("leaf", None),
        P("leaf", "grid", None),
    )
    return jax.shard_map(
        body,
        mesh=mesh,
        in_specs=placed,
        out_specs=(P("leaf", "grid", None), P("leaf", "grid", None), P("leaf", "grid", None)),
        check_vma=False,
    )
```

profile of v0, /device:TPU:0, one launch (start us, length us, event | category | flops | bytes accessed | tf_op | source)
XLA Modules:
  0.0 85.9 jit_solution(1391319304822525056)
XLA Ops:
  7.2 0.0 all-gather.2.cloned.1.call-start
  7.2 0.9 %fusion.4 = f32[1,256]{1,0:T(1,128)S(1)} fusion(s32[256]{0:T(256)S(1)} %and_select_fusion, s32[1,1,4]{2,1,0:T(1,128)} %param.7), kind=kOutput, calls=%fused_computation.9 | convolution fusion | flops 3076 | bytes 2064 | tf_op jit(solution)/shard_map/dot_general | solution.py:24
  8.1 1.8 %bitcast_select_fusion.2 = bf16[256,512]{1,0:T(8,128)(2,1)} fusion(bf16[1,256,512]{2,1,0:T(8,128)(2,1)} %param.6, pred[256]{0:T(512)(128)(4,1)S(1)} %broadcast_compare_fusion), kind=kLoop, calls=%fused_computation.7 | loop fusion | flops 131072 | bytes 524544 | tf_op jit(solution)/shard_map/jit(_where)/select_n | solution.py:28
  9.9 0.0 all-gather.2.cloned.1.call-update
  9.9 0.6 collective-permute-start
  10.5 0.7 compare_bitcast_fusion
  11.1 0.1 broadcast_bitcast_fusion
  11.2 1.8 %collective-permute-done = bf16[1,256,2048]{2,1,0:T(8,128)(2,1)S(1)} collective-permute-done((bf16[1,256,2048]{2,1,0:T(8,128)(2,1)}, bf16[1,256,2048]{2,1,0:T(8,128)(2,1)S(1)}, u32[]{:S(2)}, u32[]{:S(2)}) %collective-permute-start) | collective-permute-done | bytes 1048608 | tf_op jit(solution)/shard_map/ppermute | solution.py:10
  13.0 49.6 %all-gather.2.cloned.1.call-done = bf16[2048,512]{1,0:T(8,128)(2,1)} async-done(((bf16[256,512]{1,0:T(8,128)(2,1)}), bf16[2048,512]{1,0:T(8,128)(2,1)}) %all-gather.2.cloned.1.call-update) | async-done | bytes 2097168 | tf_op jit(solution)/shard_map/all_gather | solution.py:29
  62.5 2.7 %fusion = bf16[256,512]{1,0:T(8,128)(2,1)S(1)} fusion(bf16[2048,512]{1,0:T(8,128)(2,1)} %all-gather.2.cloned.1.call-done, bf16[1,256,2048]{2,1,0:T(8,128)(2,1)} %param.5, bf16[1,256,2048]{2,1,0:T(8,128)(2,1)S(1)} %collective-permute-done, pred[2048]{0:T(1024)(128)(4,1)S(1)} %bitcast.40), kind=kOutput, calls=%fused_computation.1 | convolution fusion | flops 537657344 | bytes 4458496 | tf_op jit(solution)/shard_map/dot_general | solution.py:30
  65.2 0.0 copy-start.1
  65.2 0.0 copy-start
  65.2 0.0 copy-start.2
  65.2 0.1 copy.11
  65.4 11.6 %all_to_all.19 = bf16[8,64,256]{2,1,0:T(8,128)(2,1)S(1)} all-to-all(bf16[8,64,256]{2,1,0:T(8,128)(2,1)S(1)} %bitcast.37), channel_id=1, replica_groups=mesh['leaf'=4,'grid'=8] {'grid'}, dimensions={0} | all-to-all | bytes 524288 | tf_op jit(solution)/shard_map/all_to_all | solution.py:31
  76.9 0.1 copy.12
  77.1 0.8 broadcast_in_dim.31
  77.9 0.0 copy-done
  77.9 0.0 copy-done.2
  77.9 1.1 %fusion.1 = f32[1,64,512]{2,1,0:T(8,128)} fusion(bf16[64,2048]{1,0:T(8,128)(2,1)S(1)} %bitcast.36, bf16[2048,512]{1,0:T(8,128)(2,1)S(1)} %copy-done, f32[1,64,512]{2,1,0:T(8,128)S(1)} %copy-done.2), kind=kOutput, calls=%fused_computation.3 | convolution fusion | flops 134250496 | bytes 2621440 | tf_op jit(solution)/shard_map/dot_general | solution.py:32
  79.1 0.0 copy-done.1
  (4 shorter events, 0.0 us)
Async XLA Ops:
  7.2 55.3 %all-gather.2.cloned.1.call-start = ((), (), s32[]{:S(2)}) async-start(), calls=%async_computation.1 | async-start | bytes 2359296 | tf_op jit(solution)/shard_map/all_gather | solution.py:29
  9.9 3.1 %collective-permute-start = (bf16[1,256,2048]{2,1,0:T(8,128)(2,1)}, bf16[1,256,2048]{2,1,0:T(8,128)(2,1)S(1)}, u32[]{:S(2)}, u32[]{:S(2)}) collective-permute-start(bf16[1,256,2048]{2,1,0:T(8,128)(2,1)} %param.5), channel_id=1, source_target_pairs={{0,8},{8,0},{16,24},{24,16},{1,9},{9,1},{17,25},{25,17},{2,10},{10... | collective-permute-start | bytes 3145736 | tf_op jit(solution)/shard_map/ppermute | solution.py:10
  65.2 13.9 %copy-start.1 = (bf16[256,512]{1,0:T(8,128)(2,1)}, bf16[256,512]{1,0:T(8,128)(2,1)S(1)}, u32[]{:S(2)}) copy-start(bf16[256,512]{1,0:T(8,128)(2,1)S(1)} %fusion) | copy-start | bytes 786436
  65.2 12.7 %copy-start = (bf16[2048,512]{1,0:T(8,128)(2,1)S(1)}, bf16[2048,512]{1,0:T(8,128)(2,1)}, u32[]{:S(2)}) copy-start(bf16[2048,512]{1,0:T(8,128)(2,1)} %all-gather.2.cloned.1.call-done) | copy-start | bytes 6291460
  65.2 12.7 %copy-start.2 = (f32[1,64,512]{2,1,0:T(8,128)S(1)}, f32[1,64,512]{2,1,0:T(8,128)}, u32[]{:S(2)}) copy-start(f32[1,64,512]{2,1,0:T(8,128)} %param.9) | copy-start | bytes 393220
Sparse Core Ops, SparseCore 0:
  10.7 51.7 all-gather.1
where the time goes:
time: 86.2 us; the launch traced here: 85.9 us
  waiting for transfers between devices  51.3 us (60%)
  between operations  14.1 us (16%)
  blocking collectives  11.6 us (13%)
  matrix products  4.67 us (5%)
  other arithmetic  2.44 us (3%)
  local copies, waits for them, and re-layouts  1.23 us (1%)
    all_gather x1, waiting for transfers between devices, body(): whole_panel = lax.all_gather(masked, 'grid', axis=0, tiled=True)  49.6 us
    all_to_all x1, blocking collectives, body(): lax.all_to_all(panel.T, 'grid', split_axis=0, concat_axis=1, tiled=True)  11.6 us
    dot_general x1, matrix products, body(): jnp.dot(mixed, whole_panel, preferred_element_type=jnp.float32)  2.66 us
    select_n x1, other arithmetic, body(): jnp.where(flags_wide > 0.5, l_panel[0], jnp.zeros((), jnp.bfloat16))  1.76 us
    ppermute x1, waiting for transfers between devices, swapped(): lax.ppermute(array, axis, [(i, i ^ 1 << stride) for i in range(lax.axis_s...  1.75 us
  transfers between devices with their start and end apart: 2, of which 2 were waited for; matrix products, arithmetic and copies ran while one was open for 1% of the time, Pallas kernels for 0%

commit v1 on v0

v1 whole, which is shorter than its diff:
```python
import functools

import jax
import jax.numpy as jnp
from jax import lax
from jax.experimental import pallas as pl
from jax.experimental.pallas import tpu as pltpu
from jax.sharding import PartitionSpec as P

B = 512
MESH = pl.DeviceIdType.MESH
FULL_K = 2048


def kernel(
    n, slices, mask_ref, owner_ref, ainv_ref, lp_ref, dinv_ref,
    panel_ref, upper_ref, diag_ref,
    sib, whole, flipped,
    sib_send, sib_recv, x_send, up_send, down_send, recv, flip_send, flip_recv,
):
    leaf, me = lax.axis_index("leaf"), lax.axis_index("grid")
    z, x = lax.div(me, 2), lax.rem(me, 2)
    line = n // 2
    partner = 2 * z + (1 - x)
    above, below = jnp.minimum(me + 2, n - 1), jnp.maximum(me - 2, 0)
    has_up, has_down = z < line - 1, z > 0
    sibling = leaf + 1 - 2 * lax.rem(leaf, 2)
    rows, depth = ainv_ref.shape[1], ainv_ref.shape[2]
    width = lp_ref.shape[2]
    cols = width // slices
    out_rows = dinv_ref.shape[1]
    per_slice = cols // out_rows
    balance = line >= 4

    barrier = pltpu.get_barrier_semaphore()

    def greet(where):
        pl.semaphore_signal(barrier, inc=1, device_id=where, device_id_type=MESH)

    greet((sibling, me))
    greet((leaf, partner))

    @pl.when(has_up)
    def _():
        greet((leaf, above))

    @pl.when(has_down)
    def _():
        greet((leaf, below))

    pl.semaphore_wait(barrier, 4 - (z == 0).astype(jnp.int32) - (z == line - 1).astype(jnp.int32))

    def part(ref, j, h):
        start = j * rows if isinstance(j, int) else pl.multiple_of(j * rows, rows)
        return ref.at[pl.ds(start, rows), pl.ds(h * cols, cols)]

    def send(j, h, sems, to, mine=False):
        src = lp_ref.at[0, :, pl.ds(h * cols, cols)] if mine else part(whole, j, h)
        return pltpu.make_async_remote_copy(
            src_ref=src, dst_ref=part(whole, j, h), send_sem=sems.at[j, h],
            recv_sem=recv.at[j, h], device_id=(leaf, to), device_id_type=MESH)

    def arrived(j, h):
        pltpu.make_async_remote_copy(
            src_ref=part(whole, j, h), dst_ref=part(whole, j, h), send_sem=x_send.at[j, h],
            recv_sem=recv.at[j, h], device_id=(leaf, partner), device_id_type=MESH).wait_recv()

    def half(h):
        return h % 2 == 0

    def moved_below(d, h):
        if not balance or d != 1:
            return False
        return (z == 1) | (z == line - 1) if half(h) else z == 1

    def moved_above(d, h):
        if not balance or d != 1:
            return False
        return (z == line - 2) | (z == 0) if half(h) else z == line - 2

    def turn_up(h):
        return (z == 0) | (z == line - 2) if half(h) else z == 0

    def turn_down(h):
        return (z == line - 1) | (z == 1) if half(h) else z == line - 1

    def own(h, act):
        act(send(me, h, x_send, partner, True))

        @pl.when(has_up)
        def _():
            act(send(me, h, up_send, above, True))

        @pl.when(has_down)
        def _():
            act(send(me, h, down_send, below, True))

    def turn(h, act):
        if not balance:
            return

        @pl.when(turn_up(h))
        def _():
            act(send(partner, h, up_send, above))

        @pl.when(turn_down(h))
        def _():
            act(send(partner, h, down_send, below))

    def relay_up(h, d, act, wait):
        j = me - 2 * d

        @pl.when(z - d >= 0)
        def _():
            if wait:
                arrived(j, h)

            @pl.when(has_up)
            def _():
                act(send(j, h, up_send, above))

            @pl.when(jnp.logical_not(moved_below(d, h)))
            def _():
                act(send(j, h, x_send, partner))

    def relay_down(h, d, act, wait):
        j = me + 2 * d

        @pl.when(z + d < line)
        def _():
            if wait:
                arrived(j, h)

            @pl.when(has_down)
            def _():
                act(send(j, h, down_send, below))

            @pl.when(jnp.logical_not(moved_above(d, h)))
            def _():
                act(send(j, h, x_send, partner))

    start, done = (lambda c: c.start()), (lambda c: c.wait_send())

    def flip(d):
        return pltpu.make_async_remote_copy(
            src_ref=flipped.at[d], dst_ref=upper_ref.at[0, :, pl.ds(pl.multiple_of(me * rows, rows), rows)],
            send_sem=flip_send.at[d], recv_sem=flip_recv.at[me],
            device_id=(leaf, d), device_id_type=MESH)

    swap = pltpu.make_async_remote_copy(
        src_ref=ainv_ref.at[0], dst_ref=sib, send_sem=sib_send, recv_sem=sib_recv,
        device_id=(sibling, me), device_id_type=MESH)

    tile = min(FULL_K, depth)

    def product(left, h):
        def step(i, total):
            k = pl.ds(pl.multiple_of(i * tile, tile), tile)
            return total + jnp.dot(left[:, k], whole[k, pl.ds(h * cols, cols)],
                                   preferred_element_type=jnp.float32)
        if depth == tile:
            return jnp.dot(left[...], whole[:, pl.ds(h * cols, cols)],
                           preferred_element_type=jnp.float32)
        return lax.fori_loop(0, depth // tile, step, jnp.zeros((rows, cols), jnp.float32))

    def finish(h):
        for d in range(1, line):
            @pl.when(z - d >= 0)
            def _():
                arrived(partner - 2 * d, h)

            @pl.when(z + d < line)
            def _():
                arrived(partner + 2 * d, h)
        panel = (-product(sib, h)).astype(jnp.bfloat16)
        turned = panel.astype(jnp.float32).T.reshape(per_slice, out_rows, rows)
        flipped[pl.ds(h * per_slice, per_slice)] = turned.astype(jnp.bfloat16)
        panel_ref[0, :, pl.ds(h * cols, cols)] = panel
        for d in range(h * per_slice, (h + 1) * per_slice):
            @pl.when(me != d)
            def _():
                flip(d).start()

            @pl.when(me == d)
            def _():
                upper_ref[0, :, pl.ds(pl.multiple_of(me * rows, rows), rows)] = flipped[d]

    order = list(range(slices))
    if slices > 2:
        order = [0, slices - 1] + list(range(1, slices - 1))

    own(order[0], start)
    if slices > 1:
        own(order[1], start)
    swap.start()
    whole[pl.ds(pl.multiple_of(me * rows, rows), rows), :] = lp_ref[0]

    for step in range(1, slices + line - 1):
        for d in range(1, line):
            i = step - d
            if not 0 <= i < slices:
                continue
            h = order[i]
            if d == 1:
                arrived(partner, h)
                turn(h, start)
            relay_up(h, d, start, True)
            relay_down(h, d, start, True)
        if step + 1 < slices:
            own(order[step + 1], start)
        if step == 1:
            swap.wait_recv()

            def mix(b, carry):
                k = pl.ds(pl.multiple_of(b * B, B), B)
                kept = jnp.where(owner_ref[0, b] == 1, sib[:, k], ainv_ref[0, :, k])
                sib[:, k] = jnp.where(mask_ref[0, 0, b] == 1, kept, jnp.zeros_like(kept))
                return carry

            lax.fori_loop(0, depth // B, mix, 0)
        i = step - (line - 1)
        if 0 <= i < slices:
            finish(order[i])

    for j in range(n):
        @pl.when(me != j)
        def _():
            pltpu.make_async_remote_copy(
                src_ref=flipped.at[0], dst_ref=upper_ref.at[0, :, pl.ds(j * rows, rows)],
                send_sem=flip_send.at[0], recv_sem=flip_recv.at[j],
                device_id=(leaf, partner), device_id_type=MESH).wait_recv()

    def update(b, total):
        k = pl.ds(pl.multiple_of(b * B, B), B)
        u = upper_ref[0, :, k]
        u = jnp.where(mask_ref[0, 0, b] == 1, u, jnp.zeros_like(u))
        return total - jnp.dot(u, whole[k, :], preferred_element_type=jnp.float32)

    diag_ref[0] = lax.fori_loop(0, depth // B, update, dinv_ref[0], unroll=depth <= tile)

    swap.wait_send()
    for h in range(slices):
        own(h, done)
        turn(h, done)
        for d in range(1, line):
            relay_up(h, d, done, False)
            relay_down(h, d, done, False)
    for d in range(n):
        @pl.when(me != d)
        def _():
            flip(d).wait_send()


def solution(mesh):
    n = mesh.shape["grid"]
    slices = 4 if n <= 16 else 1

    def body(ainv_sep, l_panel, block_mask, owner, dinv):
        rows, depth = ainv_sep.shape[1:]
        width = l_panel.shape[2]
        out_rows = dinv.shape[1]
        vmem = pl.BlockSpec(memory_space=pltpu.VMEM)
        smem = pl.BlockSpec(memory_space=pltpu.SMEM)
        dma = pltpu.SemaphoreType.DMA
        return pl.pallas_call(
            functools.partial(kernel, n, slices),
            out_shape=(
                jax.ShapeDtypeStruct((1, rows, width), jnp.bfloat16),
                jax.ShapeDtypeStruct((1, out_rows, depth), jnp.bfloat16),
                jax.ShapeDtypeStruct((1, out_rows, width), jnp.float32),
            ),
            in_specs=[smem, smem, vmem, vmem, vmem],
            out_specs=(vmem, vmem, vmem),
            scratch_shapes=[
                pltpu.VMEM((rows, depth), jnp.bfloat16),
                pltpu.VMEM((depth, width), jnp.bfloat16),
                pltpu.VMEM((n, out_rows, rows), jnp.bfloat16),
                dma, dma,
                dma((n, slices)), dma((n, slices)), dma((n, slices)), dma((n, slices)),
                dma((n,)), dma((n,)),
            ],
            compiler_params=pltpu.CompilerParams(collective_id=0, has_side_effects=True),
        )(block_mask, owner, ainv_sep, l_panel, dinv)

    placed = (
        P("leaf", "grid", None),
        P("leaf", "grid", None),
        P("leaf", None, None),
        P("leaf", None),
        P("leaf", "grid", None),
    )
    return jax.shard_map(
        body,
        mesh=mesh,
        in_specs=placed,
        out_specs=(P("leaf", "grid", None), P("leaf", "grid", None), P("leaf", "grid", None)),
        check_vma=False,
    )
```

time: 86.2 us -> 47.7 us (0.55)
  waiting for transfers between devices: 51.3 us -> 0 us
  Pallas kernels: 0 us -> 42.8 us
  between operations: 14.1 us -> 0.65 us
  blocking collectives: 11.6 us -> 0 us
  matrix products: 4.67 us -> 0 us
  other arithmetic: 2.44 us -> 0 us
  local copies, waits for them, and re-layouts: 1.23 us -> 3.37 us
    all_gather x1 -> x0, waiting for transfers between devices: 49.6 us -> none  [body(): whole_panel = lax.all_gather(masked, 'grid', axis=0, tiled=True)]
    pallas_call x0 -> x1, Pallas kernels: none -> 42.8 us  [body(): pl.pallas_call(functools.partial(kernel, n, slices), out_shape=(jax.Shape...]
    all_to_all x1 -> x0, blocking collectives: 11.6 us -> none  [body(): lax.all_to_all(panel.T, 'grid', split_axis=0, concat_axis=1, tiled=True)]
    dot_general x3 -> x0, matrix products: 4.67 us -> none  [the longest x1 2.66 us: body(): jnp.dot(mixed, whole_panel, preferred_element_type=jnp.float32)]
    unnamed x8 -> x7, local copies, waits for them, and re-layouts: 0.1 us -> 3.37 us
    select_n x2 -> x0, other arithmetic: 1.78 us -> none  [the longest x1 1.76 us: body(): jnp.where(flags_wide > 0.5, l_panel[0], jnp.zeros((), jnp.bfloat16))]
    ppermute x1 -> x0, waiting for transfers between devices: 1.75 us -> none  [swapped(): lax.ppermute(array, axis, [(i, i ^ 1 << stride) for i in range(lax.axis_s...]
  transfers between devices with their start and end apart: 2 -> 0, of which waited for: 2 -> 0; matrix products, arithmetic and copies ran while one was open for 1% -> 0% of each run, Pallas kernels for 0% -> 0%
where the time goes in v1:
time: 47.7 us; the launch traced here: 46.8 us
  Pallas kernels  42.8 us (90%)
  local copies, waits for them, and re-layouts  3.37 us (7%)
  between operations  0.65 us (1%)
    pallas_call x1, Pallas kernels, body(): pl.pallas_call(functools.partial(kernel, n, slices), out_shape=(jax.Shape...  42.8 us
    unnamed x7, local copies, waits for them, and re-layouts  3.37 us

profile of v1, /device:TPU:0, one launch (start us, length us, event | category | flops | bytes accessed | tf_op | source)
XLA Modules:
  0.0 46.8 jit_solution(9571558677091984595)
XLA Ops:
  0.6 42.8 %shard_map.76 = (bf16[1,256,512]{2,1,0:T(8,128)(2,1)}, bf16[1,64,2048]{2,1,0:T(8,128)(2,1)}, f32[1,64,512]{2,1,0:T(8,128)}) custom-call(s32[1,1,4]{2,1,0:T(1,128)} %mask_ref.1, s32[1,4]{1,0:T(1,128)} %owner_ref.1, bf16[1,256,2048]{2,1,0:T(8,128)(2,1)} %ainv_ref.1, bf16[1,256,512]{2,1,0:T(8,128)(2,1)} %lp_ref.1, f32[1,64,512]{2,1,0:T(8,128)} %dinv_ref.1), custom_call_target="tpu_custom_call" | custom-call | tf_op jit(solution)/shard_map/pallas_call | solution.py:265
  43.5 0.0 copy-start
  43.5 1.7 %copy.11 = bf16[1,256,512]{2,1,0:T(8,128)(2,1)} copy(bf16[1,256,512]{2,1,0:T(8,128)(2,1)} %get-tuple-element.6) | data formatting | bytes 524288
  45.2 0.0 copy-done
  45.2 0.0 copy-start.1
  45.2 0.7 %copy.12 = bf16[1,64,2048]{2,1,0:T(8,128)(2,1)} copy(bf16[1,64,2048]{2,1,0:T(8,128)(2,1)S(1)} %copy-done) | data formatting | bytes 524288
  45.9 0.3 copy-done.1
  46.2 0.7 %copy.13 = f32[1,64,512]{2,1,0:T(8,128)} copy(f32[1,64,512]{2,1,0:T(8,128)S(1)} %copy-done.1) | data formatting | bytes 262144
Async XLA Ops:
  43.5 1.7 %copy-start = (bf16[1,64,2048]{2,1,0:T(8,128)(2,1)S(1)}, bf16[1,64,2048]{2,1,0:T(8,128)(2,1)}, u32[]{:S(2)}) copy-start(bf16[1,64,2048]{2,1,0:T(8,128)(2,1)} %get-tuple-element.7) | copy-start | bytes 786436
  45.2 1.0 %copy-start.1 = (f32[1,64,512]{2,1,0:T(8,128)S(1)}, f32[1,64,512]{2,1,0:T(8,128)}, u32[]{:S(2)}) copy-start(f32[1,64,512]{2,1,0:T(8,128)} %get-tuple-element.8) | copy-start | bytes 393220

commit v2 on v1

--- a/solution.py
+++ b/solution.py
@@ -15,8 +15,9 @@
 def kernel(
     n, slices, mask_ref, owner_ref, ainv_ref, lp_ref, dinv_ref,
     panel_ref, upper_ref, diag_ref,
-    sib, whole, flipped,
+    sib, held, whole, flipped, masked,
     sib_send, sib_recv, x_send, up_send, down_send, recv, flip_send, flip_recv,
+    load_sem, keep_sem,
 ):
     leaf, me = lax.axis_index("leaf"), lax.axis_index("grid")
     z, x = lax.div(me, 2), lax.rem(me, 2)
@@ -30,7 +31,10 @@
     cols = width // slices
     out_rows = dinv_ref.shape[1]
     per_slice = cols // out_rows
-    balance = line >= 4
+    balance = False
+
+    def part(ref, j, h):
+        return ref.at[j, h]
 
     barrier = pltpu.get_barrier_semaphore()
 
@@ -48,16 +52,19 @@
     def _():
         greet((leaf, below))
 
+    def load(h):
+        return pltpu.make_async_copy(
+            lp_ref.at[0, :, pl.ds(h * cols, cols)], part(whole, me, h), load_sem.at[h])
+
+    for h in range(slices):
+        load(h).start()
+    keep = pltpu.make_async_copy(ainv_ref.at[0], held, keep_sem)
+    keep.start()
     pl.semaphore_wait(barrier, 4 - (z == 0).astype(jnp.int32) - (z == line - 1).astype(jnp.int32))
 
-    def part(ref, j, h):
-        start = j * rows if isinstance(j, int) else pl.multiple_of(j * rows, rows)
-        return ref.at[pl.ds(start, rows), pl.ds(h * cols, cols)]
-
-    def send(j, h, sems, to, mine=False):
-        src = lp_ref.at[0, :, pl.ds(h * cols, cols)] if mine else part(whole, j, h)
+    def send(j, h, sems, to):
         return pltpu.make_async_remote_copy(
-            src_ref=src, dst_ref=part(whole, j, h), send_sem=sems.at[j, h],
+            src_ref=part(whole, j, h), dst_ref=part(whole, j, h), send_sem=sems.at[j, h],
             recv_sem=recv.at[j, h], device_id=(leaf, to), device_id_type=MESH)
 
     def arrived(j, h):
@@ -85,15 +92,15 @@
         return (z == line - 1) | (z == 1) if half(h) else z == line - 1
 
     def own(h, act):
-        act(send(me, h, x_send, partner, True))
+        act(send(me, h, x_send, partner))
 
         @pl.when(has_up)
         def _():
-            act(send(me, h, up_send, above, True))
+            act(send(me, h, up_send, above))
 
         @pl.when(has_down)
         def _():
-            act(send(me, h, down_send, below, True))
+            act(send(me, h, down_send, below))
 
     def turn(h, act):
         if not balance:
@@ -151,17 +158,20 @@
         src_ref=ainv_ref.at[0], dst_ref=sib, send_sem=sib_send, recv_sem=sib_recv,
         device_id=(sibling, me), device_id_type=MESH)
 
-    tile = min(FULL_K, depth)
-
-    def product(left, h):
+    tile = min(FULL_K // rows, n)
+
+    def columns(i, h):
+        block = whole[pl.ds(i * tile, tile), h]
+        return block.reshape(tile * rows, cols)
+
+    def across(left, h, total):
         def step(i, total):
-            k = pl.ds(pl.multiple_of(i * tile, tile), tile)
-            return total + jnp.dot(left[:, k], whole[k, pl.ds(h * cols, cols)],
-                                   preferred_element_type=jnp.float32)
-        if depth == tile:
-            return jnp.dot(left[...], whole[:, pl.ds(h * cols, cols)],
-                           preferred_element_type=jnp.float32)
-        return lax.fori_loop(0, depth // tile, step, jnp.zeros((rows, cols), jnp.float32))
+            k = pl.ds(pl.multiple_of(i * (tile * rows), tile * rows), tile * rows)
+            return total + jnp.dot(left[:, k], columns(i, h), preferred_element_type=jnp.float32)
+
+        if tile == n:
+            return step(0, total)
+        return lax.fori_loop(0, n // tile, step, total)
 
     def finish(h):
         for d in range(1, line):
@@ -172,7 +182,7 @@
             @pl.when(z + d < line)
             def _():
                 arrived(partner + 2 * d, h)
-        panel = (-product(sib, h)).astype(jnp.bfloat16)
+        panel = (-across(sib, h, jnp.zeros((rows, cols), jnp.float32))).astype(jnp.bfloat16)
         turned = panel.astype(jnp.float32).T.reshape(per_slice, out_rows, rows)
         flipped[pl.ds(h * per_slice, per_slice)] = turned.astype(jnp.bfloat16)
         panel_ref[0, :, pl.ds(h * cols, cols)] = panel
@@ -189,38 +199,31 @@
     if slices > 2:
         order = [0, slices - 1] + list(range(1, slices - 1))
 
-    own(order[0], start)
-    if slices > 1:
-        own(order[1], start)
+    for h in order:
+        load(h).wait()
+        own(h, start)
     swap.start()
-    whole[pl.ds(pl.multiple_of(me * rows, rows), rows), :] = lp_ref[0]
-
-    for step in range(1, slices + line - 1):
-        for d in range(1, line):
-            i = step - d
-            if not 0 <= i < slices:
-                continue
-            h = order[i]
+
+    for d in range(1, line):
+        for h in order:
             if d == 1:
                 arrived(partner, h)
                 turn(h, start)
             relay_up(h, d, start, True)
             relay_down(h, d, start, True)
-        if step + 1 < slices:
-            own(order[step + 1], start)
-        if step == 1:
-            swap.wait_recv()
-
-            def mix(b, carry):
-                k = pl.ds(pl.multiple_of(b * B, B), B)
-                kept = jnp.where(owner_ref[0, b] == 1, sib[:, k], ainv_ref[0, :, k])
-                sib[:, k] = jnp.where(mask_ref[0, 0, b] == 1, kept, jnp.zeros_like(kept))
-                return carry
-
-            lax.fori_loop(0, depth // B, mix, 0)
-        i = step - (line - 1)
-        if 0 <= i < slices:
-            finish(order[i])
+
+    swap.wait_recv()
+    keep.wait()
+
+    def mix(b, carry):
+        k = pl.ds(pl.multiple_of(b * B, B), B)
+        kept = jnp.where(owner_ref[0, b] == 1, sib[:, k], held[:, k])
+        sib[:, k] = jnp.where(mask_ref[0, 0, b] == 1, kept, jnp.zeros_like(kept))
+        return carry
+
+    lax.fori_loop(0, depth // B, mix, 0)
+    for h in order:
+        finish(h)
 
     for j in range(n):
         @pl.when(me != j)
@@ -230,13 +233,17 @@
                 send_sem=flip_send.at[0], recv_sem=flip_recv.at[j],
                 device_id=(leaf, partner), device_id_type=MESH).wait_recv()
 
-    def update(b, total):
+    def sift(b, carry):
         k = pl.ds(pl.multiple_of(b * B, B), B)
         u = upper_ref[0, :, k]
-        u = jnp.where(mask_ref[0, 0, b] == 1, u, jnp.zeros_like(u))
-        return total - jnp.dot(u, whole[k, :], preferred_element_type=jnp.float32)
-
-    diag_ref[0] = lax.fori_loop(0, depth // B, update, dinv_ref[0], unroll=depth <= tile)
+        masked[:, k] = jnp.where(mask_ref[0, 0, b] == 1, u, jnp.zeros_like(u))
+        return carry
+
+    lax.fori_loop(0, depth // B, sift, 0)
+    for h in range(slices):
+        c = pl.ds(h * cols, cols)
+        update = across(masked, h, jnp.zeros((out_rows, cols), jnp.float32))
+        diag_ref[0, :, c] = dinv_ref[0, :, c] - update
 
     swap.wait_send()
     for h in range(slices):
@@ -251,6 +258,17 @@
             flip(d).wait_send()
 
 
+def write_out(panel, upper, diag, panel_out, upper_out, diag_out, *sems):
+    copies = [
+        pltpu.make_async_copy(src, dst, sem)
+        for src, dst, sem in zip((panel, upper, diag), (panel_out, upper_out, diag_out), sems)
+    ]
+    for copy in copies:
+        copy.start()
+    for copy in copies:
+        copy.wait()
+
+
 def solution(mesh):
     n = mesh.shape["grid"]
     slices = 4 if n <= 16 else 1
@@ -261,26 +279,37 @@
         out_rows = dinv.shape[1]
         vmem = pl.BlockSpec(memory_space=pltpu.VMEM)
         smem = pl.BlockSpec(memory_space=pltpu.SMEM)
+        hbm = pl.BlockSpec(memory_space=pl.ANY)
         dma = pltpu.SemaphoreType.DMA
-        return pl.pallas_call(
+        results = pl.pallas_call(
             functools.partial(kernel, n, slices),
             out_shape=(
-                jax.ShapeDtypeStruct((1, rows, width), jnp.bfloat16),
-                jax.ShapeDtypeStruct((1, out_rows, depth), jnp.bfloat16),
-                jax.ShapeDtypeStruct((1, out_rows, width), jnp.float32),
+                pltpu.VMEM((1, rows, width), jnp.bfloat16),
+                pltpu.VMEM((1, out_rows, depth), jnp.bfloat16),
+                pltpu.VMEM((1, out_rows, width), jnp.float32),
             ),
-            in_specs=[smem, smem, vmem, vmem, vmem],
+            in_specs=[smem, smem, hbm, hbm, vmem],
             out_specs=(vmem, vmem, vmem),
             scratch_shapes=[
                 pltpu.VMEM((rows, depth), jnp.bfloat16),
-                pltpu.VMEM((depth, width), jnp.bfloat16),
+                pltpu.VMEM((rows, depth), jnp.bfloat16),
+                pltpu.VMEM((n, slices, rows, width // slices), jnp.bfloat16),
                 pltpu.VMEM((n, out_rows, rows), jnp.bfloat16),
+                pltpu.VMEM((out_rows, depth), jnp.bfloat16),
                 dma, dma,
                 dma((n, slices)), dma((n, slices)), dma((n, slices)), dma((n, slices)),
                 dma((n,)), dma((n,)),
+                dma((slices,)), dma,
             ],
             compiler_params=pltpu.CompilerParams(collective_id=0, has_side_effects=True),
         )(block_mask, owner, ainv_sep, l_panel, dinv)
+        return pl.pallas_call(
+            write_out,
+            out_shape=tuple(jax.ShapeDtypeStruct(r.shape, r.dtype) for r in results),
+            in_specs=[vmem] * 3,
+            out_specs=(hbm,) * 3,
+            scratch_shapes=[dma, dma, dma],
+        )(*results)
 
     placed = (
         P("leaf", "grid", None),

time: 47.7 us -> 39.6 us (0.83)
  the two profiles are of different devices: /device:TPU:0 before, /device:TPU:22 now
where the time goes in v2:
time: 39.6 us; the launch traced here: 39.4 us
  Pallas kernels  36.8 us (93%)
  local copies, waits for them, and re-layouts  2.01 us (5%)
  between operations  0.65 us (2%)
    pallas_call x1, Pallas kernels, body(): pl.pallas_call(functools.partial(kernel, n, slices), out_shape=(pltpu.VME...  34.8 us
    unnamed x6, local copies, waits for them, and re-layouts  2.01 us
    pallas_call x1, Pallas kernels, body(): pl.pallas_call(write_out, out_shape=tuple((jax.ShapeDtypeStruct(r.shape,...  1.91 us

profile of v2, /device:TPU:22, one launch (start us, length us, event | category | flops | bytes accessed | tf_op | source)
XLA Modules:
  0.0 39.4 jit_solution(16259932355048092885)
XLA Ops:
  0.6 34.8 %shard_map.76 = (bf16[1,256,512]{2,1,0:T(8,128)(2,1)S(1)}, bf16[1,64,2048]{2,1,0:T(8,128)(2,1)S(1)}, f32[1,64,512]{2,1,0:T(8,128)S(1)}) custom-call(s32[1,1,4]{2,1,0:T(1,128)} %mask_ref.1, s32[1,4]{1,0:T(1,128)} %owner_ref.1, bf16[1,256,2048]{2,1,0:T(8,128)(2,1)} %ainv_ref.1, bf16[1,256,512]{2,1,0:T(8,128)(2,1)} %lp_ref.1, f32[1,64,512]{2,1,0:T(8,128)} %dinv_ref.1), custom_call_target="tpu_custom_call" | custom-call | tf_op jit(solution)/shard_map/pallas_call | solution.py:284
  35.5 0.0 copy-start
  35.5 0.7 %copy-done = bf16[1,256,512]{2,1,0:T(8,128)(2,1)} copy-done((bf16[1,256,512]{2,1,0:T(8,128)(2,1)}, bf16[1,256,512]{2,1,0:T(8,128)(2,1)S(1)}, u32[]{:S(2)}) %copy-start) | copy-done | bytes 262168
  36.2 0.0 copy-start.1
  36.2 0.7 %copy-done.1 = bf16[1,64,2048]{2,1,0:T(8,128)(2,1)} copy-done((bf16[1,64,2048]{2,1,0:T(8,128)(2,1)}, bf16[1,64,2048]{2,1,0:T(8,128)(2,1)S(1)}, u32[]{:S(2)}) %copy-start.1) | copy-done | bytes 262168
  36.9 0.0 copy-start.2
  36.9 0.6 %copy-done.2 = f32[1,64,512]{2,1,0:T(8,128)} copy-done((f32[1,64,512]{2,1,0:T(8,128)}, f32[1,64,512]{2,1,0:T(8,128)S(1)}, u32[]{:S(2)}) %copy-start.2) | copy-done | bytes 131096
  37.5 1.9 %shard_map.77 = (bf16[1,256,512]{2,1,0:T(8,128)(2,1)}, bf16[1,64,2048]{2,1,0:T(8,128)(2,1)}, f32[1,64,512]{2,1,0:T(8,128)}) custom-call(bf16[1,256,512]{2,1,0:T(8,128)(2,1)} %copy-done, bf16[1,64,2048]{2,1,0:T(8,128)(2,1)} %copy-done.1, f32[1,64,512]{2,1,0:T(8,128)} %copy-done.2), custom_call_target="tpu_custom_call" | custom-call | tf_op jit(solution)/shard_map/pallas_call | solution.py:306
Async XLA Ops:
  35.5 0.7 %copy-start = (bf16[1,256,512]{2,1,0:T(8,128)(2,1)}, bf16[1,256,512]{2,1,0:T(8,128)(2,1)S(1)}, u32[]{:S(2)}) copy-start(bf16[1,256,512]{2,1,0:T(8,128)(2,1)S(1)} %get-tuple-element.6.panel) | copy-start | bytes 786436
  36.2 0.7 %copy-start.1 = (bf16[1,64,2048]{2,1,0:T(8,128)(2,1)}, bf16[1,64,2048]{2,1,0:T(8,128)(2,1)S(1)}, u32[]{:S(2)}) copy-start(bf16[1,64,2048]{2,1,0:T(8,128)(2,1)S(1)} %get-tuple-element.7.upper) | copy-start | bytes 786436
  36.9 0.6 %copy-start.2 = (f32[1,64,512]{2,1,0:T(8,128)}, f32[1,64,512]{2,1,0:T(8,128)S(1)}, u32[]{:S(2)}) copy-start(f32[1,64,512]{2,1,0:T(8,128)S(1)} %get-tuple-element.8.diag) | copy-start | bytes 393220

commit v3 on v2

--- a/solution.py
+++ b/solution.py
@@ -17,7 +17,7 @@
     panel_ref, upper_ref, diag_ref,
     sib, held, whole, flipped, masked,
     sib_send, sib_recv, x_send, up_send, down_send, recv, flip_send, flip_recv,
-    load_sem, keep_sem,
+    load_sem, keep_sem, base, base_sem, mask, owners, mask_sem, owner_sem,
 ):
     leaf, me = lax.axis_index("leaf"), lax.axis_index("grid")
     z, x = lax.div(me, 2), lax.rem(me, 2)
@@ -31,7 +31,7 @@
     cols = width // slices
     out_rows = dinv_ref.shape[1]
     per_slice = cols // out_rows
-    balance = False
+    balance = line >= 4
 
     def part(ref, j, h):
         return ref.at[j, h]
@@ -60,6 +60,12 @@
         load(h).start()
     keep = pltpu.make_async_copy(ainv_ref.at[0], held, keep_sem)
     keep.start()
+    initial = pltpu.make_async_copy(dinv_ref.at[0], base, base_sem)
+    initial.start()
+    flags = pltpu.make_async_copy(mask_ref, mask, mask_sem)
+    flags.start()
+    owned = pltpu.make_async_copy(owner_ref, owners, owner_sem)
+    owned.start()
     pl.semaphore_wait(barrier, 4 - (z == 0).astype(jnp.int32) - (z == line - 1).astype(jnp.int32))
 
     def send(j, h, sems, to):
@@ -85,11 +91,15 @@
             return False
         return (z == line - 2) | (z == 0) if half(h) else z == line - 2
 
-    def turn_up(h):
-        return (z == 0) | (z == line - 2) if half(h) else z == 0
-
-    def turn_down(h):
-        return (z == line - 1) | (z == 1) if half(h) else z == line - 1
+    def turn_up(h, early):
+        if early:
+            return z == 0
+        return z == line - 2 if half(h) else None
+
+    def turn_down(h, early):
+        if early:
+            return z == line - 1
+        return z == 1 if half(h) else None
 
     def own(h, act):
         act(send(me, h, x_send, partner))
@@ -102,15 +112,15 @@
         def _():
             act(send(me, h, down_send, below))
 
-    def turn(h, act):
-        if not balance:
+    def turn(h, act, early):
+        if not balance or turn_up(h, early) is None:
             return
 
-        @pl.when(turn_up(h))
+        @pl.when(turn_up(h, early))
         def _():
             act(send(partner, h, up_send, above))
 
-        @pl.when(turn_down(h))
+        @pl.when(turn_down(h, early))
         def _():
             act(send(partner, h, down_send, below))
 
@@ -208,17 +218,22 @@
         for h in order:
             if d == 1:
                 arrived(partner, h)
-                turn(h, start)
+                turn(h, start, True)
             relay_up(h, d, start, True)
             relay_down(h, d, start, True)
 
+    for h in order:
+        turn(h, start, False)
     swap.wait_recv()
     keep.wait()
+    initial.wait()
+    flags.wait()
+    owned.wait()
 
     def mix(b, carry):
         k = pl.ds(pl.multiple_of(b * B, B), B)
-        kept = jnp.where(owner_ref[0, b] == 1, sib[:, k], held[:, k])
-        sib[:, k] = jnp.where(mask_ref[0, 0, b] == 1, kept, jnp.zeros_like(kept))
+        kept = jnp.where(owners[0, b] == 1, sib[:, k], held[:, k])
+        sib[:, k] = jnp.where(mask[0, 0, b] == 1, kept, jnp.zeros_like(kept))
         return carry
 
     lax.fori_loop(0, depth // B, mix, 0)
@@ -236,19 +251,20 @@
     def sift(b, carry):
         k = pl.ds(pl.multiple_of(b * B, B), B)
         u = upper_ref[0, :, k]
-        masked[:, k] = jnp.where(mask_ref[0, 0, b] == 1, u, jnp.zeros_like(u))
+        masked[:, k] = jnp.where(mask[0, 0, b] == 1, u, jnp.zeros_like(u))
         return carry
 
     lax.fori_loop(0, depth // B, sift, 0)
     for h in range(slices):
         c = pl.ds(h * cols, cols)
         update = across(masked, h, jnp.zeros((out_rows, cols), jnp.float32))
-        diag_ref[0, :, c] = dinv_ref[0, :, c] - update
+        diag_ref[0, :, c] = base[:, c] - update
 
     swap.wait_send()
     for h in range(slices):
         own(h, done)
-        turn(h, done)
+        turn(h, done, True)
+        turn(h, done, False)
         for d in range(1, line):
             relay_up(h, d, done, False)
             relay_down(h, d, done, False)
@@ -256,17 +272,6 @@
         @pl.when(me != d)
         def _():
             flip(d).wait_send()
-
-
-def write_out(panel, upper, diag, panel_out, upper_out, diag_out, *sems):
-    copies = [
-        pltpu.make_async_copy(src, dst, sem)
-        for src, dst, sem in zip((panel, upper, diag), (panel_out, upper_out, diag_out), sems)
-    ]
-    for copy in copies:
-        copy.start()
-    for copy in copies:
-        copy.wait()
 
 
 def solution(mesh):
@@ -288,7 +293,7 @@
                 pltpu.VMEM((1, out_rows, depth), jnp.bfloat16),
                 pltpu.VMEM((1, out_rows, width), jnp.float32),
             ),
-            in_specs=[smem, smem, hbm, hbm, vmem],
+            in_specs=[hbm] * 5,
             out_specs=(vmem, vmem, vmem),
             scratch_shapes=[
                 pltpu.VMEM((rows, depth), jnp.bfloat16),
@@ -300,16 +305,12 @@
                 dma((n, slices)), dma((n, slices)), dma((n, slices)), dma((n, slices)),
                 dma((n,)), dma((n,)),
                 dma((slices,)), dma,
+                pltpu.VMEM((out_rows, width), jnp.float32), dma,
+                pltpu.SMEM(block_mask.shape, jnp.int32), pltpu.SMEM(owner.shape, jnp.int32), dma, dma,
             ],
             compiler_params=pltpu.CompilerParams(collective_id=0, has_side_effects=True),
         )(block_mask, owner, ainv_sep, l_panel, dinv)
-        return pl.pallas_call(
-            write_out,
-            out_shape=tuple(jax.ShapeDtypeStruct(r.shape, r.dtype) for r in results),
-            in_specs=[vmem] * 3,
-            out_specs=(hbm,) * 3,
-            scratch_shapes=[dma, dma, dma],
-        )(*results)
+        return tuple(results)
 
     placed = (
         P("leaf", "grid", None),

time: 39.6 us -> 36.5 us (0.922)
  the two profiles are of different devices: /device:TPU:22 before, /device:TPU:0 now
where the time goes in v3:
time: 36.5 us; the launch traced here: 36.4 us
  Pallas kernels  33.7 us (92%)
  local copies, waits for them, and re-layouts  2.06 us (6%)
  between operations  0.64 us (2%)
    pallas_call x1, Pallas kernels, body(): pl.pallas_call(functools.partial(kernel, n, slices), out_shape=(pltpu.VME...  33.7 us
    unnamed x3, local copies, waits for them, and re-layouts  2.06 us

profile of v3, /device:TPU:0, one launch (start us, length us, event | category | flops | bytes accessed | tf_op | source)
XLA Modules:
  0.0 36.4 jit_solution(10586773019424879362)
XLA Ops:
  0.6 33.7 %shard_map.76 = (bf16[1,256,512]{2,1,0:T(8,128)(2,1)S(1)}, bf16[1,64,2048]{2,1,0:T(8,128)(2,1)S(1)}, f32[1,64,512]{2,1,0:T(8,128)S(1)}) custom-call(s32[1,1,4]{2,1,0:T(1,128)} %mask_ref.1, s32[1,4]{1,0:T(1,128)} %owner_ref.1, bf16[1,256,2048]{2,1,0:T(8,128)(2,1)} %ainv_ref.1, bf16[1,256,512]{2,1,0:T(8,128)(2,1)} %lp_ref.1, f32[1,64,512]{2,1,0:T(8,128)} %dinv_ref.1), custom_call_target="tpu_custom_call" | custom-call | tf_op jit(solution)/shard_map/pallas_call | solution.py:289
  34.3 0.7 %copy.11 = bf16[1,256,512]{2,1,0:T(8,128)(2,1)} copy(bf16[1,256,512]{2,1,0:T(8,128)(2,1)S(1)} %get-tuple-element.3) | data formatting | bytes 524288
  35.0 0.7 %copy.13 = f32[1,64,512]{2,1,0:T(8,128)} copy(f32[1,64,512]{2,1,0:T(8,128)S(1)} %get-tuple-element.5) | data formatting | bytes 262144
  35.7 0.7 %copy.12 = bf16[1,64,2048]{2,1,0:T(8,128)(2,1)} copy(bf16[1,64,2048]{2,1,0:T(8,128)(2,1)S(1)} %get-tuple-element.4) | data formatting | bytes 524288
